TPU v7x, 32 devices: a whole 2x2x4 slice. The times are simulated.
32 devices in a mesh: row: 4 (over z), col: 4 (over y, x), layer: 2 (over core).
Axes of the slice: x: 2, y: 2, z: 4, core: 2. Of those that a mesh axis runs over, the one named last changes fastest.
Arguments:
- wavefunction: float32 [4096, 4096], P('row', 'col'), may hold values from -0.015625 to 1.515625
- start_block: float32 [4096, 2048], P(('col', 'layer'), 'row'), may hold values from -6 to 6
Outputs:
- basis: float32 [4096, 2048], P(('col', 'layer'), 'row')
All inputs are finite; a program needn't handle non-finite values.
Results may differ from a plain program's by a relative error of at most 0.0003.
Values sent between devices are 32-bit elements; how exact they have to be, the bound alone decides.
No kernel may reach another device: no remote copies, remote signals or barrier semaphores. Data moves between devices by JAX's collectives and lax.ppermute only.
A program may use at most 128 MiB of HBM per device.

v0:
```python
import math
import jax
import jax.numpy as jnp
from jax import lax
from jax.sharding import PartitionSpec as P


def spread(x, axis, root):
    mine = lax.axis_index(axis) == root
    return lax.psum(jnp.where(mine, x, jnp.zeros_like(x)), axis)


def cross(left, right):
    return lax.dot_general(
        left,
        right,
        (((0,), (0,)), ((), ())),
        precision=lax.Precision.HIGHEST,
        preferred_element_type=jnp.float32,
    )


def times(left, right):
    return jnp.dot(left, right, precision=lax.Precision.HIGHEST, preferred_element_type=jnp.float32)


def apply_density(rho_slab, basis_block):
    return lax.psum_scatter(
        cross(rho_slab, basis_block), ("col", "layer"), scatter_dimension=0, tiled=True
    )


def orthonormalize(image_block):
    panel_owner = lax.axis_index("row")
    panels = lax.axis_size("row")
    current = image_block
    gram_matrix = lax.psum(cross(current, current), ("col", "layer"))
    for panel_index in range(panels):
        factor = jnp.linalg.cholesky(gram_matrix)
        new_basis = jax.scipy.linalg.solve_triangular(factor, current.T, lower=True).T
        current = jnp.where(panel_owner == panel_index, new_basis, current)
        if panel_index + 1 < panels:
            chosen = spread(current, "row", panel_index)
            later = panel_owner > panel_index
            correlation, square = lax.psum(
                (cross(chosen, current), cross(current, current)), ("col", "layer")
            )
            current = jnp.where(later, current - times(chosen, correlation), current)
            gram_matrix = jnp.where(later, square - cross(correlation, correlation), square)
    return current


def shards(wavefunction, start_block):
    layers = lax.axis_size("layer")
    column_width = wavefunction.shape[1] // layers
    own_slice = lax.dynamic_slice_in_dim(
        wavefunction, lax.axis_index("layer") * column_width, column_width, 1
    )
    own_rows = lax.all_gather(own_slice, "col", axis=1, tiled=True)
    partner = spread(own_rows, "row", lax.axis_index("col"))
    rho_part = lax.psum_scatter(
        lax.dot_general(
            partner,
            own_rows,
            (((1,), (1,)), ((), ())),
            precision=lax.Precision.HIGHEST,
            preferred_element_type=jnp.float32,
        ),
        "layer",
        scatter_dimension=0,
        tiled=True,
    )
    rho_slab = lax.all_gather(rho_part, "row", axis=1, tiled=True)
    current = start_block
    image_block = apply_density(rho_slab, current)
    current = orthonormalize(image_block)
    return current * math.sqrt(rho_slab.shape[1])


def solution(mesh):
    placed = (P("row", "col"), P(("col", "layer"), "row"))
    return jax.shard_map(
        shards, mesh=mesh, in_specs=placed, out_specs=P(("col", "layer"), "row"), check_vma=False
    )
```

profile of v0, /device:TPU:0, one launch (start us, length us, event | category | flops | bytes accessed | tf_op | source)
XLA Modules:
  0.0 1721.6 jit_solution(5460350467099761118)
XLA Ops:
  9.9 90.3 %all-gather.3.cloned.1.call-done = f32[1024,2048]{1,0:T(8,128)} async-done(((f32[1024,512]{1,0:T(8,128)}), f32[1024,2048]{1,0:T(8,128)}) %all-gather.3.cloned.1.call-update) | async-done | bytes 8388624 | tf_op jit(solution)/shard_map/all_gather | solution.py:59
  108.5 290.9 %all-reduce.13.cloned.1.call-done = f32[1024,2048]{1,0:T(8,128)} async-done(((f32[1024,2048]{1,0:T(8,128)}), f32[1024,2048]{1,0:T(8,128)}) %all-reduce.13.cloned.1.call-update) | async-done | bytes 8388624 | tf_op jit(solution)/shard_map/psum | solution.py:10
  399.4 32.1 %fusion.156 = f32[1024,1024]{1,0:T(8,128)} fusion(f32[1024,2048]{1,0:T(8,128)} %all-reduce.13.cloned.1.call-done, f32[1024,2048]{1,0:T(8,128)} %all-gather.3.cloned.1.call-done), kind=kOutput, calls=%fused_computation.284 | convolution fusion | flops 25769803776 | bytes 20971520 | tf_op jit(solution)/shard_map/dot_general | solution.py:62
  431.6 11.1 reduce-scatter.3.cloned.1.call-done
  443.1 152.0 %all-gather.5.cloned.1.call-done = f32[512,4096]{1,0:T(8,128)} async-done(((f32[512,1024]{1,0:T(8,128)}), f32[512,4096]{1,0:T(8,128)}) %all-gather.5.cloned.1.call-update) | async-done | bytes 8388624 | tf_op jit(solution)/shard_map/all_gather | solution.py:73
  595.1 17.1 fusion.157
  612.2 69.6 %reduce-scatter.5.cloned.1.call-done = f32[512,512]{0,1:T(8,128)} async-done(((f32[4096,512]{0,1:T(8,128)}), f32[512,512]{0,1:T(8,128)}) %reduce-scatter.5.cloned.1.call-update) | async-done | bytes 1048592 | tf_op jit(solution)/shard_map/reduce_scatter | solution.py:28
  686.9 56.3 %all-reduce.15.cloned.1.call-done = f32[512,512]{0,1:T(8,128)} async-done(((f32[512,512]{0,1:T(8,128)}), f32[512,512]{0,1:T(8,128)}) %all-reduce.15.cloned.1.call-update) | async-done | bytes 1048592 | tf_op jit(solution)/shard_map/psum | solution.py:37
  746.2 11.7 cholesky.462
  757.9 9.8 custom-call.35
  768.6 11.7 cholesky.481
  780.3 10.0 custom-call.36
  790.9 11.7 cholesky.502
  803.4 9.8 custom-call.37
  813.8 11.7 cholesky.519
  838.3 39.3 %custom-call.38 = f32[4,128,128]{1,2,0:T(8,128)S(1)} custom-call(f32[4,128,128]{2,1,0:T(8,128)S(1)} %get-tuple-element.33), custom_call_target="InvertDiagBlocksLowerTriangular" | custom-call | tf_op jit(solution)/shard_map/jit(_solve_triangular)/triangular_solve | solution.py:40
  884.9 48.4 %all-reduce.17.cloned.1.call-done = f32[512,512]{0,1:T(8,128)} async-done(((f32[512,512]{0,1:T(8,128)}), f32[512,512]{0,1:T(8,128)}) %all-reduce.17.cloned.1.call-update) | async-done | bytes 1048592 | tf_op jit(solution)/shard_map/psum | solution.py:10
  937.8 60.8 %all-reduce.27.cloned.1.call-done = (f32[512,512]{1,0:T(8,128)}, f32[512,512]{0,1:T(8,128)}) async-done(((f32[512,512]{1,0:T(8,128)}, f32[512,512]{0,1:T(8,128)}), (f32[512,512]{1,0:T(8,128)}, f32[512,512]{0,1:T(8,128)})) %all-reduce.27.cloned.1.call-update) | async-done | bytes 2097168 | tf_op jit(solution)/shard_map/psum | solution.py:45
  1006.3 11.7 cholesky.534
  1018.2 9.8 custom-call.39
  1030.6 11.9 cholesky.553
  1043.8 9.8 custom-call.40
  1055.2 11.7 cholesky.574
  1067.6 9.8 custom-call.41
  1078.8 12.1 cholesky.591
  1095.2 11.4 while.9
  1106.6 39.3 %custom-call.42 = f32[4,128,128]{1,2,0:T(8,128)S(1)} custom-call(f32[4,128,128]{2,1,0:T(8,128)S(1)} %get-tuple-element.34), custom_call_target="InvertDiagBlocksLowerTriangular" | custom-call | tf_op jit(solution)/shard_map/jit(_solve_triangular)/triangular_solve | solution.py:40
  1159.0 48.2 %all-reduce.19.cloned.1.call-done = f32[512,512]{0,1:T(8,128)} async-done(((f32[512,512]{0,1:T(8,128)}), f32[512,512]{0,1:T(8,128)}) %all-reduce.19.cloned.1.call-update) | async-done | bytes 1048592 | tf_op jit(solution)/shard_map/psum | solution.py:10
  1211.5 61.1 %all-reduce.25.cloned.1.call-done = (f32[512,512]{1,0:T(8,128)}, f32[512,512]{0,1:T(8,128)}) async-done(((f32[512,512]{1,0:T(8,128)}, f32[512,512]{0,1:T(8,128)}), (f32[512,512]{1,0:T(8,128)}, f32[512,512]{0,1:T(8,128)})) %all-reduce.25.cloned.1.call-update) | async-done | bytes 2097168 | tf_op jit(solution)/shard_map/psum | solution.py:45
  1280.2 11.7 cholesky.606
  1292.1 9.8 custom-call.43
  1304.5 11.9 cholesky.625
  1317.7 9.8 custom-call.44
  1329.1 11.7 cholesky.646
  1341.5 9.8 custom-call.45
  1352.8 12.1 cholesky.663
  1369.2 11.4 while.10
  1380.5 39.3 %custom-call.46 = f32[4,128,128]{1,2,0:T(8,128)S(1)} custom-call(f32[4,128,128]{2,1,0:T(8,128)S(1)} %get-tuple-element.35), custom_call_target="InvertDiagBlocksLowerTriangular" | custom-call | tf_op jit(solution)/shard_map/jit(_solve_triangular)/triangular_solve | solution.py:40
  1433.1 48.0 %all-reduce.21.cloned.1.call-done = f32[512,512]{0,1:T(8,128)} async-done(((f32[512,512]{0,1:T(8,128)}), f32[512,512]{0,1:T(8,128)}) %all-reduce.21.cloned.1.call-update) | async-done | bytes 1048592 | tf_op jit(solution)/shard_map/psum | solution.py:10
  1485.2 61.3 %all-reduce.23.cloned.1.call-done = (f32[512,512]{1,0:T(8,128)}, f32[512,512]{0,1:T(8,128)}) async-done(((f32[512,512]{1,0:T(8,128)}, f32[512,512]{0,1:T(8,128)}), (f32[512,512]{1,0:T(8,128)}, f32[512,512]{0,1:T(8,128)})) %all-reduce.23.cloned.1.call-update) | async-done | bytes 2097168 | tf_op jit(solution)/shard_map/psum | solution.py:45
  1554.2 11.7 cholesky.678
  1567.0 10.0 custom-call.47
  1580.2 11.7 cholesky.697
  1606.0 11.7 cholesky.718
  1619.1 10.2 custom-call.49
  1631.5 11.7 cholesky.735
  1650.2 13.7 while.11
  1663.9 40.1 %custom-call.50 = f32[4,128,128]{1,2,0:T(8,128)S(1)} custom-call(f32[4,128,128]{2,1,0:T(8,128)} %get-tuple-element.36), custom_call_target="InvertDiagBlocksLowerTriangular" | custom-call | tf_op jit(solution)/shard_map/jit(_solve_triangular)/triangular_solve | solution.py:40
  (229 shorter events, 202.7 us)
Async XLA Ops:
  6.5 588.5 %copy-start = (f32[512,512]{1,0:T(8,128)S(1)}, f32[512,512]{1,0:T(8,128)}, u32[]{:S(2)}) copy-start(f32[512,512]{1,0:T(8,128)} %param.6) | copy-start | bytes 3145732
  6.5 93.6 %all-gather.3.cloned.1.call-start = ((), (), s32[]{:S(2)}) async-start(), calls=%async_computation.2 | async-start | bytes 10485760 | tf_op jit(solution)/shard_map/all_gather | solution.py:59
  9.8 389.6 %all-reduce.13.cloned.1.call-start = ((), (), s32[]{:S(2)}) async-start(), calls=%async_computation.3 | async-start | bytes 16777216 | tf_op jit(solution)/shard_map/psum | solution.py:10
  108.4 334.3 %reduce-scatter.3.cloned.1.call-start = ((), (), s32[]{:S(2)}) async-start(), calls=%async_computation.4 | async-start | bytes 6291456 | tf_op jit(solution)/shard_map/reduce_scatter | solution.py:61
  431.5 163.5 %all-gather.5.cloned.1.call-start = ((), (), s32[]{:S(2)}) async-start(), calls=%async_computation.5 | async-start | bytes 10485760 | tf_op jit(solution)/shard_map/all_gather | solution.py:73
  442.7 239.1 %reduce-scatter.5.cloned.1.call-start = ((), (), s32[]{:S(2)}) async-start(), calls=%async_computation.6 | async-start | bytes 9437184 | tf_op jit(solution)/shard_map/reduce_scatter | solution.py:28
  612.2 131.0 %all-reduce.15.cloned.1.call-start = ((), (), s32[]{:S(2)}) async-start(), calls=%async_computation.7 | async-start | bytes 2097152 | tf_op jit(solution)/shard_map/psum | solution.py:37
  681.8 195.8 %copy-start.2 = (f32[512,512]{0,1:T(8,128)S(1)}, f32[512,512]{0,1:T(8,128)}, u32[]{:S(2)}) copy-start(f32[512,512]{0,1:T(8,128)} %reduce-scatter.5.cloned.1.call-done) | copy-start | bytes 3145732
  686.3 247.0 %all-reduce.17.cloned.1.call-start = ((), (), s32[]{:S(2)}) async-start(), calls=%async_computation.8 | async-start | bytes 2097152 | tf_op jit(solution)/shard_map/psum | solution.py:10
  882.0 116.7 %all-reduce.27.cloned.1.call-start = ((), (), s32[]{:S(2)}) async-start(), calls=%async_computation.13 | async-start | bytes 4194304 | tf_op jit(solution)/shard_map/psum | solution.py:45
  937.4 269.8 %all-reduce.19.cloned.1.call-start = ((), (), s32[]{:S(2)}) async-start(), calls=%async_computation.9 | async-start | bytes 2097152 | tf_op jit(solution)/shard_map/psum | solution.py:10
  998.7 147.3 %copy-start.4 = (f32[512,512]{1,0:T(8,128)S(1)}, f32[512,512]{1,0:T(8,128)}, u32[]{:S(2)}) copy-start(f32[512,512]{1,0:T(8,128)} %get-tuple-element.73) | copy-start | bytes 3145732
  1005.4 1.0 copy-start.6
  1156.1 116.5 %all-reduce.25.cloned.1.call-start = ((), (), s32[]{:S(2)}) async-start(), calls=%async_computation.12 | async-start | bytes 4194304 | tf_op jit(solution)/shard_map/psum | solution.py:45
  1211.3 269.9 %all-reduce.21.cloned.1.call-start = ((), (), s32[]{:S(2)}) async-start(), calls=%async_computation.10 | async-start | bytes 2097152 | tf_op jit(solution)/shard_map/psum | solution.py:10
  1272.6 147.3 %copy-start.5 = (f32[512,512]{1,0:T(8,128)S(1)}, f32[512,512]{1,0:T(8,128)}, u32[]{:S(2)}) copy-start(f32[512,512]{1,0:T(8,128)} %get-tuple-element.71) | copy-start | bytes 3145732
  1279.3 1.0 copy-start.7
  1430.1 116.5 %all-reduce.23.cloned.1.call-start = ((), (), s32[]{:S(2)}) async-start(), calls=%async_computation.11 | async-start | bytes 4194304 | tf_op jit(solution)/shard_map/psum | solution.py:45
  1546.5 157.5 %copy-start.3 = (f32[512,512]{1,0:T(8,128)S(1)}, f32[512,512]{1,0:T(8,128)}, u32[]{:S(2)}) copy-start(f32[512,512]{1,0:T(8,128)} %get-tuple-element.69) | copy-start | bytes 3145732
  1553.2 1.0 copy-start.8
  1647.0 67.5 %copy-start.1 = (f32[512,512]{1,0:T(8,128)S(1)}, f32[512,512]{1,0:T(8,128)}, u32[]{:S(2)}) copy-start(f32[512,512]{1,0:T(8,128)} %param.6) | copy-start | bytes 3145732
Sparse Core Ops, SparseCore 0:
  9.9 90.1 all-gather.2
  108.5 290.8 all-reduce.12
  431.7 10.9 reduce-scatter.2
  444.1 150.8 all-gather.4
  612.3 69.4 reduce-scatter.4
  686.4 56.6 all-reduce.14
  882.1 51.1 all-reduce.16
  937.5 61.1 all-reduce.26
  1156.2 50.9 all-reduce.18
  1211.4 61.1 all-reduce.24
  1430.2 50.9 all-reduce.20
  1485.3 61.1 all-reduce.22
where the time goes:
time: 1730 us; the launch traced here: 1720 us
  waiting for transfers between devices  998 us (58%)
  other arithmetic  500 us (29%)
  matrix products  136 us (8%)
  local copies, waits for them, and re-layouts  59.8 us (3%)
  between operations  24.6 us (1%)
    psum x4, waiting for transfers between devices, spread(): return lax.psum(jnp.where(mine, x, jnp.zeros_like(x)), axis)  436 us
    another operation x59, other arithmetic, orthonormalize(): factor = jnp.linalg.cholesky(gram_matrix)  319 us
    psum x3, waiting for transfers between devices, orthonormalize(): lax.psum((cross(chosen, current), cross(current, current)), ('col', 'laye...  183 us
    another operation x9, other arithmetic, orthonormalize(): jax.scipy.linalg.solve_triangular(factor, current.T, lower=True)  163 us
    all_gather x1, waiting for transfers between devices, shards(): rho_slab = lax.all_gather(rho_part, 'row', axis=1, tiled=True)  152 us
    all_gather x1, waiting for transfers between devices, shards(): own_rows = lax.all_gather(own_slice, 'col', axis=1, tiled=True)  90.3 us
    reduce_scatter x1, waiting for transfers between devices, apply_density(): lax.psum_scatter(cross(rho_slab, basis_block), ('col', 'layer'), scatter_...  69.6 us
    psum x1, waiting for transfers between devices, orthonormalize(): gram_matrix = lax.psum(cross(current, current), ('col', 'layer'))  56.3 us
  transfers between devices with their start and end apart: 12, of which 12 were waited for; matrix products, arithmetic and copies ran while one was open for 0% of the time, Pallas kernels for 0%

commit v1 on v0

--- a/solution.py
+++ b/solution.py
@@ -7,7 +7,7 @@
 
 def spread(x, axis, root):
     mine = lax.axis_index(axis) == root
-    return lax.psum(jnp.where(mine, x, jnp.zeros_like(x)), axis)
+    return jnp.sum(lax.all_gather(jnp.where(mine, x, jnp.zeros_like(x)), axis), axis=0)
 
 
 def cross(left, right):

time: 1730 us -> 2100 us (1.21)
  waiting for transfers between devices: 998 us -> 1350 us
    all_gather x0 -> x4, waiting for transfers between devices: none -> 793 us  [spread(): lax.all_gather(jnp.where(mine, x, jnp.zeros_like(x)), axis)]
    psum x4 -> x0, waiting for transfers between devices: 436 us -> none  [spread(): return lax.psum(jnp.where(mine, x, jnp.zeros_like(x)), axis)]
    reduce_sum x0 -> x4, other arithmetic: none -> 30 us  [spread(): jnp.sum(lax.all_gather(jnp.where(mine, x, jnp.zeros_like(x)), axis), axis=0)]
where the time goes in v1:
time: 2100 us; the launch traced here: 2090 us
  waiting for transfers between devices  1350 us (64%)
  other arithmetic  520 us (25%)
  matrix products  126 us (6%)
  local copies, waits for them, and re-layouts  65.6 us (3%)
  between operations  24.8 us (1%)
    all_gather x4, waiting for transfers between devices, spread(): lax.all_gather(jnp.where(mine, x, jnp.zeros_like(x)), axis)  793 us
    another operation x59, other arithmetic, orthonormalize(): factor = jnp.linalg.cholesky(gram_matrix)  317 us
    psum x3, waiting for transfers between devices, orthonormalize(): lax.psum((cross(chosen, current), cross(current, current)), ('col', 'laye...  181 us
    another operation x9, other arithmetic, orthonormalize(): jax.scipy.linalg.solve_triangular(factor, current.T, lower=True)  159 us
    all_gather x1, waiting for transfers between devices, shards(): rho_slab = lax.all_gather(rho_part, 'row', axis=1, tiled=True)  152 us
    all_gather x1, waiting for transfers between devices, shards(): own_rows = lax.all_gather(own_slice, 'col', axis=1, tiled=True)  90.3 us
    reduce_scatter x1, waiting for transfers between devices, apply_density(): lax.psum_scatter(cross(rho_slab, basis_block), ('col', 'layer'), scatter_...  69.6 us
    psum x1, waiting for transfers between devices, orthonormalize(): gram_matrix = lax.psum(cross(current, current), ('col', 'layer'))  56.8 us
  transfers between devices with their start and end apart: 12, of which 12 were waited for; matrix products, arithmetic and copies ran while one was open for 0% of the time, Pallas kernels for 0%

profile of v1, /device:TPU:0, one launch (start us, length us, event | category | flops | bytes accessed | tf_op | source)
XLA Modules:
  0.0 2090.6 jit_solution(3396753527094381356)
XLA Ops:
  9.8 90.3 %all-gather.11.cloned.1.call-done = f32[1024,2048]{1,0:T(8,128)} async-done(((f32[1024,512]{1,0:T(8,128)}), f32[1024,2048]{1,0:T(8,128)}) %all-gather.11.cloned.1.call-update) | async-done | bytes 8388624 | tf_op jit(solution)/shard_map/all_gather | solution.py:59
  108.4 561.5 %all-gather.15.cloned.1.call-done = f32[4096,2048]{1,0:T(8,128)} async-done(((f32[1024,2048]{1,0:T(8,128)}), f32[4096,2048]{1,0:T(8,128)}) %all-gather.15.cloned.1.call-update) | async-done | bytes 33554448 | tf_op jit(solution)/shard_map/all_gather | solution.py:10
  669.9 15.9 reduce_sum.36
  685.8 32.1 %fusion.156 = f32[1024,1024]{1,0:T(8,128)} fusion(f32[1024,2048]{1,0:T(8,128)} %reduce_sum.36, f32[1024,2048]{1,0:T(8,128)} %all-gather.11.cloned.1.call-done), kind=kOutput, calls=%fused_computation.284 | convolution fusion | flops 25769803776 | bytes 20971520 | tf_op jit(solution)/shard_map/dot_general | solution.py:62
  718.0 10.3 reduce-scatter.3.cloned.1.call-done
  728.6 152.1 %all-gather.13.cloned.1.call-done = f32[512,4096]{1,0:T(8,128)} async-done(((f32[512,1024]{1,0:T(8,128)}), f32[512,4096]{1,0:T(8,128)}) %all-gather.13.cloned.1.call-update) | async-done | bytes 8388624 | tf_op jit(solution)/shard_map/all_gather | solution.py:73
  880.7 17.1 fusion.157
  897.8 69.6 %reduce-scatter.5.cloned.1.call-done = f32[512,512]{0,1:T(8,128)} async-done(((f32[4096,512]{0,1:T(8,128)}), f32[512,512]{0,1:T(8,128)}) %reduce-scatter.5.cloned.1.call-update) | async-done | bytes 1048592 | tf_op jit(solution)/shard_map/reduce_scatter | solution.py:28
  972.0 56.8 %all-reduce.9.cloned.1.call-done = f32[512,512]{0,1:T(8,128)} async-done(((f32[512,512]{0,1:T(8,128)}), f32[512,512]{0,1:T(8,128)}) %all-reduce.9.cloned.1.call-update) | async-done | bytes 1048592 | tf_op jit(solution)/shard_map/psum | solution.py:37
  1031.9 11.7 cholesky.462
  1043.6 9.8 custom-call.35
  1054.2 11.7 cholesky.481
  1066.0 10.2 custom-call.36
  1076.8 11.7 cholesky.502
  1089.3 9.8 custom-call.37
  1099.7 11.7 cholesky.519
  1124.1 39.3 %custom-call.38 = f32[4,128,128]{1,2,0:T(8,128)S(1)} custom-call(f32[4,128,128]{2,1,0:T(8,128)S(1)} %get-tuple-element.33), custom_call_target="InvertDiagBlocksLowerTriangular" | custom-call | tf_op jit(solution)/shard_map/jit(_solve_triangular)/triangular_solve | solution.py:40
  1170.8 77.2 %all-gather.17.cloned.1.call-done = f32[2048,512]{0,1:T(8,128)} async-done(((f32[512,512]{0,1:T(8,128)}), f32[2048,512]{0,1:T(8,128)}) %all-gather.17.cloned.1.call-update) | async-done | bytes 4194320 | tf_op jit(solution)/shard_map/all_gather | solution.py:10
  1262.0 60.0 %all-reduce.15.cloned.1.call-done = (f32[512,512]{1,0:T(8,128)}, f32[512,512]{0,1:T(8,128)}) async-done(((f32[512,512]{1,0:T(8,128)}, f32[512,512]{0,1:T(8,128)}), (f32[512,512]{1,0:T(8,128)}, f32[512,512]{0,1:T(8,128)})) %all-reduce.15.cloned.1.call-update) | async-done | bytes 2097168 | tf_op jit(solution)/shard_map/psum | solution.py:45
  1330.5 11.7 cholesky.534
  1342.4 9.8 custom-call.39
  1354.7 11.9 cholesky.553
  1367.9 9.8 custom-call.40
  1379.3 11.7 cholesky.574
  1391.7 9.8 custom-call.41
  1403.4 11.7 cholesky.591
  1427.0 39.3 %custom-call.42 = f32[4,128,128]{1,2,0:T(8,128)S(1)} custom-call(f32[4,128,128]{2,1,0:T(8,128)S(1)} %get-tuple-element.34), custom_call_target="InvertDiagBlocksLowerTriangular" | custom-call | tf_op jit(solution)/shard_map/jit(_solve_triangular)/triangular_solve | solution.py:40
  1473.7 77.0 %all-gather.19.cloned.1.call-done = f32[2048,512]{0,1:T(8,128)} async-done(((f32[512,512]{0,1:T(8,128)}), f32[2048,512]{0,1:T(8,128)}) %all-gather.19.cloned.1.call-update) | async-done | bytes 4194320 | tf_op jit(solution)/shard_map/all_gather | solution.py:10
  1564.4 60.2 %all-reduce.13.cloned.1.call-done = (f32[512,512]{1,0:T(8,128)}, f32[512,512]{0,1:T(8,128)}) async-done(((f32[512,512]{1,0:T(8,128)}, f32[512,512]{0,1:T(8,128)}), (f32[512,512]{1,0:T(8,128)}, f32[512,512]{0,1:T(8,128)})) %all-reduce.13.cloned.1.call-update) | async-done | bytes 2097168 | tf_op jit(solution)/shard_map/psum | solution.py:45
  1633.1 11.7 cholesky.606
  1645.0 9.8 custom-call.43
  1657.3 11.9 cholesky.625
  1670.6 9.8 custom-call.44
  1682.0 11.7 cholesky.646
  1694.4 9.8 custom-call.45
  1706.0 11.7 cholesky.663
  1729.6 39.3 %custom-call.46 = f32[4,128,128]{1,2,0:T(8,128)S(1)} custom-call(f32[4,128,128]{2,1,0:T(8,128)S(1)} %get-tuple-element.35), custom_call_target="InvertDiagBlocksLowerTriangular" | custom-call | tf_op jit(solution)/shard_map/jit(_solve_triangular)/triangular_solve | solution.py:40
  1776.3 77.0 %all-gather.21.cloned.1.call-done = f32[2048,512]{0,1:T(8,128)} async-done(((f32[512,512]{0,1:T(8,128)}), f32[2048,512]{0,1:T(8,128)}) %all-gather.21.cloned.1.call-update) | async-done | bytes 4194320 | tf_op jit(solution)/shard_map/all_gather | solution.py:10
  1867.0 60.5 %all-reduce.11.cloned.1.call-done = (f32[512,512]{1,0:T(8,128)}, f32[512,512]{0,1:T(8,128)}) async-done(((f32[512,512]{1,0:T(8,128)}, f32[512,512]{0,1:T(8,128)}), (f32[512,512]{1,0:T(8,128)}, f32[512,512]{0,1:T(8,128)})) %all-reduce.11.cloned.1.call-update) | async-done | bytes 2097168 | tf_op jit(solution)/shard_map/psum | solution.py:45
  1935.9 11.9 cholesky.678
  1948.0 9.8 custom-call.47
  1960.4 11.7 cholesky.697
  1973.5 9.8 custom-call.48
  1984.9 12.1 cholesky.718
  1997.7 9.8 custom-call.49
  2008.9 11.7 cholesky.735
  2025.0 11.7 while.11
  2036.7 39.5 %custom-call.50 = f32[4,128,128]{1,2,0:T(8,128)S(1)} custom-call(f32[4,128,128]{2,1,0:T(8,128)S(1)} %get-tuple-element.36), custom_call_target="InvertDiagBlocksLowerTriangular" | custom-call | tf_op jit(solution)/shard_map/jit(_solve_triangular)/triangular_solve | solution.py:40
  (230 shorter events, 209.5 us)
Async XLA Ops:
  6.5 874.1 %copy-start = (f32[512,512]{1,0:T(8,128)S(1)}, f32[512,512]{1,0:T(8,128)}, u32[]{:S(2)}) copy-start(f32[512,512]{1,0:T(8,128)} %param.6) | copy-start | bytes 3145732
  6.5 93.6 %all-gather.11.cloned.1.call-start = ((), (), s32[]{:S(2)}) async-start(), calls=%async_computation.2 | async-start | bytes 10485760 | tf_op jit(solution)/shard_map/all_gather | solution.py:59
  9.8 660.1 %all-gather.15.cloned.1.call-start = ((), (), s32[]{:S(2)}) async-start(), calls=%async_computation.7 | async-start | bytes 41943040 | tf_op jit(solution)/shard_map/all_gather | solution.py:10
  108.3 620.0 %reduce-scatter.3.cloned.1.call-start = ((), (), s32[]{:S(2)}) async-start(), calls=%async_computation.3 | async-start | bytes 6291456 | tf_op jit(solution)/shard_map/reduce_scatter | solution.py:61
  717.9 162.7 %all-gather.13.cloned.1.call-start = ((), (), s32[]{:S(2)}) async-start(), calls=%async_computation.4 | async-start | bytes 10485760 | tf_op jit(solution)/shard_map/all_gather | solution.py:73
  728.3 239.1 %reduce-scatter.5.cloned.1.call-start = ((), (), s32[]{:S(2)}) async-start(), calls=%async_computation.5 | async-start | bytes 9437184 | tf_op jit(solution)/shard_map/reduce_scatter | solution.py:28
  897.8 131.0 %all-reduce.9.cloned.1.call-start = ((), (), s32[]{:S(2)}) async-start(), calls=%async_computation.6 | async-start | bytes 2097152 | tf_op jit(solution)/shard_map/psum | solution.py:37
  967.5 196.0 %copy-start.2 = (f32[512,512]{0,1:T(8,128)S(1)}, f32[512,512]{0,1:T(8,128)}, u32[]{:S(2)}) copy-start(f32[512,512]{0,1:T(8,128)} %reduce-scatter.5.cloned.1.call-done) | copy-start | bytes 3145732
  972.0 276.0 %all-gather.17.cloned.1.call-start = ((), (), s32[]{:S(2)}) async-start(), calls=%async_computation.8 | async-start | bytes 5242880 | tf_op jit(solution)/shard_map/all_gather | solution.py:10
  1167.9 154.2 %all-reduce.15.cloned.1.call-start = ((), (), s32[]{:S(2)}) async-start(), calls=%async_computation.13 | async-start | bytes 4194304 | tf_op jit(solution)/shard_map/psum | solution.py:45
  1261.6 289.1 %all-gather.19.cloned.1.call-start = ((), (), s32[]{:S(2)}) async-start(), calls=%async_computation.9 | async-start | bytes 5242880 | tf_op jit(solution)/shard_map/all_gather | solution.py:10
  1329.5 1.0 copy-start.3
  1470.7 154.0 %all-reduce.13.cloned.1.call-start = ((), (), s32[]{:S(2)}) async-start(), calls=%async_computation.12 | async-start | bytes 4194304 | tf_op jit(solution)/shard_map/psum | solution.py:45
  1564.2 289.1 %all-gather.21.cloned.1.call-start = ((), (), s32[]{:S(2)}) async-start(), calls=%async_computation.10 | async-start | bytes 5242880 | tf_op jit(solution)/shard_map/all_gather | solution.py:10
  1632.1 1.0 copy-start.4
  1773.3 154.1 %all-reduce.11.cloned.1.call-start = ((), (), s32[]{:S(2)}) async-start(), calls=%async_computation.11 | async-start | bytes 4194304 | tf_op jit(solution)/shard_map/psum | solution.py:45
  1934.9 1.0 copy-start.5
  1959.0 124.6 %copy-start.1 = (f32[512,512]{1,0:T(8,128)S(1)}, f32[512,512]{1,0:T(8,128)}, u32[]{:S(2)}) copy-start(f32[512,512]{1,0:T(8,128)} %param.6) | copy-start | bytes 3145732
Sparse Core Ops, SparseCore 0:
  9.9 90.1 all-gather.10
  108.5 561.3 all-gather.14
  718.1 10.2 reduce-scatter.2
  729.7 150.8 all-gather.12
  897.9 69.5 reduce-scatter.4
  972.1 56.7 all-reduce.8
  1168.0 79.9 all-gather.16
  1261.7 60.3 all-reduce.14
  1470.8 79.7 all-gather.18
  1564.3 60.3 all-reduce.12
  1773.5 79.7 all-gather.20
  1867.1 60.2 all-reduce.10
